TPU v7x, 512 devices: a whole 4x4x16 slice. The times are simulated.
512 devices in a mesh: expert: 8 (over x, core), dp: 64 (over z, y).
Axes of the slice: x: 4, y: 4, z: 16, core: 2. Of those that a mesh axis runs over, the one named last changes fastest.
Arguments:
- grads: bfloat16 [8, 64, 128, 6144], P('expert', 'dp'), may hold values from -16 to 16
- master: float32 [8, 128, 6144], P('expert', 'dp'), may hold values from -0.0625 to 0.0625
- first_moment: float32 [8, 128, 6144], P('expert', 'dp'), may hold values from -0.0029296875 to 0.0029296875
- second_moment: float32 [8, 128, 6144], P('expert', 'dp'), may hold values from 1e-08 to 1e-07
Outputs:
- new_master: float32 [8, 128, 6144], P('expert', 'dp')
- new_first: float32 [8, 128, 6144], P('expert', 'dp')
- new_second: float32 [8, 128, 6144], P('expert', 'dp')
- direction: float32 [8, 128, 6144], P('expert', 'dp')
- new_weights: bfloat16 [8, 128, 6144], P('expert')
All inputs are finite; a program needn't handle non-finite values.
Results may differ from a plain program's by a relative error of at most 0.0004.
Values may be sent and summed in bfloat16 or wider, within the bound.
A program may use at most 64 MiB of HBM per device.

v0:
```python
import jax.numpy as jnp
from jax import lax

STEP = 10


def reference(grads, master, first_moment, second_moment):

    def add_one(index, total):
        piece = lax.dynamic_index_in_dim(grads, index, 1, keepdims=False)
        return total + piece.astype(jnp.float32)

    summed = lax.fori_loop(0, grads.shape[1], add_one, jnp.zeros(master.shape, jnp.float32))
    norm = jnp.sqrt(jnp.sum(summed * summed))
    clip = 1.0 / jnp.maximum(norm, 1.0)
    clipped = clip * summed
    new_first = 0.9 * first_moment + 0.1 * clipped
    new_second = 0.95 * second_moment + 0.05 * (clipped * clipped)
    first_fix = 1.0 - 0.9**STEP
    second_fix = 1.0 - 0.95**STEP
    direction = new_first / first_fix / (jnp.sqrt(new_second / second_fix) + 1e-08)
    new_master = master - 0.001 * (direction + 0.1 * master)
    new_weights = new_master.astype(jnp.bfloat16)
    return (new_master, new_first, new_second, direction, new_weights)


def solution(mesh):
    return reference
```

profile of v0, /device:TPU:4, one launch (start us, length us, event | category | flops | bytes accessed | tf_op | source)
XLA Modules:
  0.0 362.2 jit_solution(14642019052809805684)
XLA Ops:
  7.2 4.4 %reshape.28 = bf16[1,1,64,2,6144]{4,3,1,0,2:T(2,128)(2,1)} reshape(bf16[1,1,128,6144]{3,2,1,0:T(8,128)(2,1)} %param.4) | data formatting | bytes 3145728 | tf_op jit(solution)/call_exported
  11.5 18.9 %all-to-all-start = ((bf16[1,1,64,2,6144]{4,3,1,0,2:T(2,128)(2,1)}), bf16[1,1,64,2,6144]{4,3,1,0,2:T(2,128)(2,1)S(1)}, u32[]{:S(2)}, u32[]{:S(2)}) async-start(bf16[1,1,64,2,6144]{4,3,1,0,2:T(2,128)(2,1)} %reshape.28), calls=%async_computation | async-start | bytes 3145728 | tf_op jit(solution)/call_exported
  30.5 77.7 %all-to-all-done = bf16[1,1,64,2,6144]{4,3,1,0,2:T(2,128)(2,1)S(1)} async-done(((bf16[1,1,64,2,6144]{4,3,1,0,2:T(2,128)(2,1)}), bf16[1,1,64,2,6144]{4,3,1,0,2:T(2,128)(2,1)S(1)}, u32[]{:S(2)}, u32[]{:S(2)}) %all-to-all-start) | async-done | bytes 1572896 | tf_op jit(solution)/call_exported
  108.2 4.9 %while.17 = (s32[]{:T(128)}, f32[1,2,6144]{2,1,0:T(2,128)S(1)}, bf16[1,1,128,6144]{3,2,1,0:T(8,128)(2,1)}, bf16[1,1,64,2,6144]{4,3,2,1,0:T(2,128)(2,1)S(1)}, s32[]{:T(128)}, /*index=5*/s32[]{:T(128)}) while((s32[]{:T(128)}, f32[1,2,6144]{2,1,0:T(2,128)S(1)}, bf16[1,1,128,6144]{3,2,1,0:T(8,128)(2,1)}, ...), condition=%wide.wide.region_1.2_spmd.clone, body=%wide.wide.region_0.1_spmd.clone.sunk | while | flops 36867 | bytes 122971 | solution.py:13
  108.3 0.1 convert_add_fusion.2
  108.4 0.1 convert_add_fusion.2
  108.6 0.1 convert_add_fusion.2
  108.7 0.1 convert_add_fusion.2
  108.9 0.1 convert_add_fusion.2
  109.0 0.1 convert_add_fusion.2
  109.3 0.1 convert_add_fusion.2
  109.6 0.1 convert_add_fusion.2
  110.7 0.1 convert_add_fusion.2
  111.0 0.1 convert_add_fusion.2
  111.2 0.1 convert_add_fusion.2
  111.5 0.1 convert_add_fusion.2
  112.5 0.1 convert_add_fusion.2
  112.8 0.1 convert_add_fusion.2
  113.1 0.6 multiply_reduce_fusion
  113.7 98.4 %all-reduce = f32[]{:T(128)} all-reduce(f32[]{:T(128)} %multiply_reduce_fusion), channel_id=2, replica_groups=mesh['expert'=8,'dp'=64] {'expert','dp'}, use_global_device_ids=true, to_apply=%region_2.3.clone | all-reduce | flops 1 | bytes 8 | tf_op jit(solution)/reduce_sum | solution.py:14
  212.8 0.8 fusion
  213.7 0.7 copy.15
  214.3 137.1 %all-gather.3.cloned.1.call-done = bf16[1,128,6144]{2,0,1:T(2,128)(2,1)} async-done(((bf16[1,2,6144]{2,0,1:T(2,128)(2,1)}), bf16[1,128,6144]{2,0,1:T(2,128)(2,1)}) %all-gather.3.cloned.1.call-update) | async-done | bytes 1572880 | tf_op jit(solution)/convert_element_type | solution.py:23
  351.5 3.9 %copy.16 = bf16[1,128,6144]{2,1,0:T(8,128)(2,1)} copy(bf16[1,128,6144]{2,0,1:T(2,128)(2,1)} %all-gather.3.cloned.1.call-done) | data formatting | bytes 3145728
  (59 shorter events, 3.5 us)
Async XLA Ops:
  11.5 201.3 %copy-start = (f32[1,2,6144]{2,1,0:T(2,128)S(1)}, f32[1,2,6144]{2,1,0:T(2,128)}, u32[]{:S(2)}) copy-start(f32[1,2,6144]{2,1,0:T(2,128)} %param.2) | copy-start | bytes 147460
  11.5 201.3 %copy-start.1 = (f32[1,2,6144]{2,1,0:T(2,128)S(1)}, f32[1,2,6144]{2,1,0:T(2,128)}, u32[]{:S(2)}) copy-start(f32[1,2,6144]{2,1,0:T(2,128)} %param.3) | copy-start | bytes 147460
  11.5 201.3 %copy-start.2 = (f32[1,2,6144]{2,1,0:T(2,128)S(1)}, f32[1,2,6144]{2,1,0:T(2,128)}, u32[]{:S(2)}) copy-start(f32[1,2,6144]{2,1,0:T(2,128)} %param.5) | copy-start | bytes 147460
  11.5 96.6 %all-to-all-start = ((bf16[1,1,64,2,6144]{4,3,1,0,2:T(2,128)(2,1)}), bf16[1,1,64,2,6144]{4,3,1,0,2:T(2,128)(2,1)S(1)}, u32[]{:S(2)}, u32[]{:S(2)}) async-start(bf16[1,1,64,2,6144]{4,3,1,0,2:T(2,128)(2,1)} %reshape.28), calls=%async_computation | async-start | bytes 3145728 | tf_op jit(solution)/call_exported
  30.4 321.0 %all-gather.3.cloned.1.call-start = ((), (), s32[]{:S(2)}) async-start(), calls=%async_computation.1 | async-start | bytes 3194880 | tf_op jit(solution)/convert_element_type | solution.py:23
Sparse Core Ops, SparseCore 0:
  214.5 136.9 all-gather.2
where the time goes:
time: 363 us; the launch traced here: 362 us
  waiting for transfers between devices  215 us (59%)
  blocking collectives  98.4 us (27%)
  starting transfers between devices  18.9 us (5%)
  between operations  14.8 us (4%)
  local copies, waits for them, and re-layouts  8.97 us (2%)
  other arithmetic  5.95 us (2%)
    convert_element_type x1, waiting for transfers between devices, reference(): new_weights = new_master.astype(jnp.bfloat16)  137 us
    reduce_sum x1, blocking collectives, reference(): norm = jnp.sqrt(jnp.sum(summed * summed))  98.4 us
    another operation x1, waiting for transfers between devices  77.7 us
    another operation x1, starting transfers between devices  18.9 us
  transfers between devices with their start and end apart: 2, of which 2 were waited for; matrix products, arithmetic and copies ran while one was open for 0% of the time, Pallas kernels for 0%

commit v1 on v0

v1 whole, which is shorter than its diff:
```python
import functools

import jax
import jax.numpy as jnp
from jax import lax
from jax.experimental import pallas as pl
from jax.experimental.pallas import tpu as pltpu
from jax.sharding import PartitionSpec as P

STEP = 10
NY = 4
AG_STRIDE = 2
MESH = pl.DeviceIdType.MESH


def adam(clip, summed, master, first, second):
    clipped = clip * summed
    new_first = 0.9 * first + 0.1 * clipped
    new_second = 0.95 * second + 0.05 * (clipped * clipped)
    first_fix = 1.0 - 0.9**STEP
    second_fix = 1.0 - 0.95**STEP
    direction = new_first / first_fix / (jnp.sqrt(new_second / second_fix) + 1e-08)
    new_master = master - 0.001 * (direction + 0.1 * master)
    return new_master, new_first, new_second, direction


def kernel(
    n_e, nz, quarter,
    g_hbm, master_ref, first_ref, second_ref,
    o_master, o_first, o_second, o_direction, w_ref,
    g, own_q, yin, rin, zin, zout, total_q, s_out, s_in, t_in, norm_out, n1, norm2_out, n2,
    load_sem, own_sem, y_ssem, y_rsem, r_ssem, r_rsem, z_ssem, z_rsem,
    x_ssem, x_rsem, n1_ssem, n1_rsem, n2_ssem, n2_rsem,
    az_ssem, az_rsem, ay_ssem, ay_rsem, ar_ssem, ar_rsem,
):
    half = quarter // 2
    hz = nz // 2
    e = lax.axis_index("expert")
    d = lax.axis_index("dp")
    z = d // NY
    y = d % NY

    def at(zz, yy):
        return (e, ((zz + nz) % nz) * NY + (yy + NY) % NY)

    def columns(q):
        return pl.ds(pl.multiple_of(q * quarter, 128), quarter)

    loads = []
    for i in range(NY):
        q = (y + 1 + i) % NY
        dst = g.at[:, :, pl.ds(i * quarter, quarter)] if i < NY - 1 else own_q
        copy = pltpu.make_async_copy(g_hbm.at[:, :, columns(q)], dst, load_sem.at[i])
        copy.start()
        loads.append(copy)

    barrier = pltpu.get_barrier_semaphore()
    for dz in (1, -1):
        pl.semaphore_signal(barrier, inc=1, device_id=at(z + dz, y), device_id_type=MESH)

    def greet(i, carry):
        i = i + 1
        ee = (e + i // NY) % n_e
        yy = (y + i % NY) % NY
        pl.semaphore_signal(barrier, inc=1, device_id=(ee, z * NY + yy), device_id_type=MESH)
        return carry

    lax.fori_loop(0, n_e * NY - 1, greet, 0)
    pl.semaphore_wait(barrier, n_e * NY + 1)
    for copy in loads:
        copy.wait()

    def tile(j):
        i = (j + 1) // 2
        sign = 2 * (j % 2) - 1
        return (z + 2 * nz + sign * (hz - i)) % nz

    def y_copy(way, j):
        src = g.at[tile(j), :, pl.ds(way * 3 * half, 3 * half)]
        return pltpu.make_async_remote_copy(
            src_ref=src, dst_ref=yin.at[way, j], send_sem=y_ssem.at[way, j], recv_sem=y_rsem.at[way, j],
            device_id=at(z, y + 1 - 2 * way), device_id_type=MESH)

    def relay(way, j):
        src = yin.at[way, j, :, pl.ds(2 * half if way == 0 else 0, half)]
        return pltpu.make_async_remote_copy(
            src_ref=src, dst_ref=rin.at[way, j], send_sem=r_ssem.at[way, j], recv_sem=r_rsem.at[way, j],
            device_id=at(z, y + 1 - 2 * way), device_id_type=MESH)

    def z_copy(way, i, h):
        return pltpu.make_async_remote_copy(
            src_ref=zout.at[way, i, h], dst_ref=zin.at[way, i + 1, h],
            send_sem=z_ssem.at[way, i, h], recv_sem=z_rsem.at[way, i + 1, h],
            device_id=at(z + 1 - 2 * way, y), device_id_type=MESH)

    def arrive(j):
        for way in (0, 1):
            y_copy(way, j).wait_recv()
            relay(way, j).start()

    def y_start(j):
        for way in (0, 1):
            y_copy(way, j).start()

    def y_sum(j, h):
        cols = pl.ds(h * half, half)
        own = own_q[tile(j), :, cols].astype(jnp.float32)
        left = yin[0, j, :, cols].astype(jnp.float32)
        right = yin[1, j, :, pl.ds(half + h * half, half)].astype(jnp.float32)
        far = rin[h, j].astype(jnp.float32)
        return (own + left) + (right + far)

    def z_step(i, ways, begins):
        for h in (0, 1):
            for way in ways:
                j = 0 if isinstance(i, int) and i == 0 else 2 * i - 1 + way
                relay(h, j).wait_recv()
                value = y_sum(j, h)
                if not begins[way]:
                    z_copy(way, i - 1, h).wait_recv()
                    value = value + zin[way, i, h]
                zout[way, i, h] = value
                z_copy(way, i, h).start()

    for j in (0, 1, 2):
        y_start(j)
    arrive(0)
    for j in (3, 4):
        if j < nz:
            y_start(j)
    arrive(1)
    arrive(2)
    for j in (5, 6):
        if j < nz:
            y_start(j)
    z_step(0, (0,), (True, True))
    for j in (3, 4):
        if j < nz:
            arrive(j)
    for j in (7, 8):
        if j < nz:
            y_start(j)
    z_step(1, (0, 1), (False, True))

    def middle(i, carry):
        arrive(2 * i + 1)
        pl.when(2 * i + 2 < nz)(lambda: arrive(2 * i + 2))
        pl.when(2 * i + 5 < nz)(lambda: y_start(2 * i + 5))
        pl.when(2 * i + 6 < nz)(lambda: y_start(2 * i + 6))
        z_step(i, (0, 1), (False, False))
        return carry

    lax.fori_loop(2, hz, middle, 0)

    squares = jnp.zeros((8, half), jnp.float32)
    for h in (0, 1):
        relay(h, nz - 1).wait_recv()
        value = y_sum(nz - 1, h)
        for way in (0, 1):
            z_copy(way, hz - 1, h).wait_recv()
            value = value + zin[way, hz, h]
        total_q[:, pl.ds(h * half, half)] = value
        squares = squares + value * value

    norm_out[...] = jnp.sum(jnp.sum(squares.reshape(8, half // 128, 128), axis=1), axis=0, keepdims=True)
    mine = e * NY + y
    n1[mine] = norm_out[...]

    def n1_copy(i):
        ee = (e + i // NY) % n_e
        yy = (y + i % NY) % NY
        return pltpu.make_async_remote_copy(
            src_ref=norm_out, dst_ref=n1.at[mine], send_sem=n1_ssem.at[i], recv_sem=n1_rsem.at[i],
            device_id=(ee, z * NY + yy), device_id_type=MESH)

    lax.fori_loop(1, n_e * NY, lambda i, c: (n1_copy(i).start(), c)[1], 0)

    for k in range(NY):
        s_out[k] = total_q[pl.ds(2 * k, 2), :]

    def x_copies(i):
        yy = (y + i) % NY
        copies = [pltpu.make_async_remote_copy(
            src_ref=s_out.at[yy], dst_ref=s_in.at[y], send_sem=x_ssem.at[0, i], recv_sem=x_rsem.at[0, i],
            device_id=at(z, yy), device_id_type=MESH)]
        for a, ref in enumerate((master_ref, first_ref, second_ref)):
            copies.append(pltpu.make_async_remote_copy(
                src_ref=ref.at[:, columns(yy)], dst_ref=t_in.at[a, y],
                send_sem=x_ssem.at[a + 1, i], recv_sem=x_rsem.at[a + 1, i],
                device_id=at(z, yy), device_id_type=MESH))
        return copies

    for i in range(1, NY):
        for copy in x_copies(i):
            copy.start()
    s_in[y] = s_out[y]
    for a, ref in enumerate((master_ref, first_ref, second_ref)):
        t_in[a, y] = ref[:, columns(y)]

    lax.fori_loop(1, n_e * NY, lambda i, c: (n1_copy(i).wait_recv(), c)[1], 0)
    norm2_out[...] = jnp.sum(n1[...], axis=0)
    n2[z] = norm2_out[...]

    def n2_copy(i):
        return pltpu.make_async_remote_copy(
            src_ref=norm2_out, dst_ref=n2.at[z], send_sem=n2_ssem.at[i], recv_sem=n2_rsem.at[i],
            device_id=at(z + i, y), device_id_type=MESH)

    lax.fori_loop(1, nz, lambda i, c: (n2_copy(i).start(), c)[1], 0)
    for i in range(1, NY):
        for copy in x_copies(i):
            copy.wait_recv()
    lax.fori_loop(1, nz, lambda i, c: (n2_copy(i).wait_recv(), c)[1], 0)
    norm = jnp.sqrt(jnp.sum(jnp.sum(n2[...], axis=0), axis=1, keepdims=True))
    clip = 1.0 / jnp.maximum(norm, 1.0)

    states = [jnp.concatenate([t_in[a, k] for k in range(NY)], axis=0) for a in range(3)]
    w_ref[z, :, columns(y)] = adam(clip, total_q[...], *states)[0].astype(jnp.bfloat16)

    reach = (hz, hz - 1)

    def az_copy(way, t, stride):
        sign = 1 - 2 * way
        piece = w_ref.at[(z - sign * t + nz) % nz, :, columns(y)]
        return pltpu.make_async_remote_copy(
            src_ref=piece, dst_ref=piece, send_sem=az_ssem.at[way, t + stride], recv_sem=az_rsem.at[way, t + stride],
            device_id=at(z + sign * stride, y), device_id_type=MESH)

    def az_arrived(way, t):
        sign = 1 - 2 * way
        piece = w_ref.at[(z - sign * t + nz) % nz, :, columns(y)]
        pltpu.make_async_remote_copy(
            src_ref=piece, dst_ref=piece, send_sem=az_ssem.at[way, t], recv_sem=az_rsem.at[way, t],
            device_id=at(z - sign, y), device_id_type=MESH).wait_recv()

    def ag_tile(j):
        t = (j + 1) // 2
        sign = 1 - 2 * (j % 2)
        return (z + nz + sign * t) % nz

    def ay_copy(way, j, forward):
        yy = y if forward else (y - 1 + 2 * way + NY) % NY
        piece = w_ref.at[ag_tile(j), :, columns(yy)]
        return pltpu.make_async_remote_copy(
            src_ref=piece, dst_ref=piece, send_sem=ay_ssem.at[way, j], recv_sem=ay_rsem.at[way, j],
            device_id=at(z, y + 1 - 2 * way), device_id_type=MESH)

    def ar_copy(way, j, forward):
        q = ((y - 1 + 2 * way + NY) if forward else (y + 2)) % NY
        piece = w_ref.at[ag_tile(j), :, pl.ds(pl.multiple_of(q * quarter + way * half, 128), half)]
        return pltpu.make_async_remote_copy(
            src_ref=piece, dst_ref=piece, send_sem=ar_ssem.at[way, j], recv_sem=ar_rsem.at[way, j],
            device_id=at(z, y + 1 - 2 * way), device_id_type=MESH)

    def y_out(j):
        for way in (0, 1):
            ay_copy(way, j, True).start()

    def y_relay(j):
        for way in (0, 1):
            ay_copy(way, j, False).wait_recv()
            ar_copy(way, j, True).start()

    for stride in range(1, AG_STRIDE + 1):
        for way in (0, 1):
            if stride <= reach[way]:
                az_copy(way, 0, stride).start()
    y_out(0)

    for k in range(NY):
        cols = pl.ds(k * quarter, quarter)
        got = adam(clip, s_in[k], master_ref[:, cols], first_ref[:, cols], second_ref[:, cols])
        for ref, value in zip((o_master, o_first, o_second, o_direction), got):
            ref[:, cols] = value

    for t in range(1, hz + 1):
        for way in (0, 1):
            if t <= reach[way]:
                az_arrived(way, t)
                if t + AG_STRIDE <= reach[way]:
                    az_copy(way, t, AG_STRIDE).start()
                y_out(2 * t - 1 + way)
        if t == 1:
            y_relay(0)
        else:
            y_relay(2 * t - 3)
            y_relay(2 * t - 2)
    y_relay(nz - 1)

    def finish(j, carry):
        for way in (0, 1):
            ar_copy(way, j, False).wait_recv()
            y_copy(way, j).wait_send()
            relay(way, j).wait_send()
            ay_copy(way, j, True).wait_send()
            ar_copy(way, j, True).wait_send()
        return carry

    lax.fori_loop(0, nz, finish, 0)
    for h in (0, 1):
        for way in (0, 1):
            lax.fori_loop(way, hz, lambda i, c: (z_copy(way, i, h).wait_send(), c)[1], 0)
    for way in (0, 1):
        for t in range(1, reach[way] + 1):
            az_copy(way, max(t - AG_STRIDE, 0), min(t, AG_STRIDE)).wait_send()
    lax.fori_loop(1, n_e * NY, lambda i, c: (n1_copy(i).wait_send(), c)[1], 0)
    lax.fori_loop(1, nz, lambda i, c: (n2_copy(i).wait_send(), c)[1], 0)
    for i in range(1, NY):
        for copy in x_copies(i):
            copy.wait_send()


def solution(mesh):
    n_e = mesh.shape["expert"]
    nz = mesh.shape["dp"] // NY

    def step(grads, master, first, second):
        rows, width = grads.shape[2:]
        quarter = width // NY
        half = quarter // 2
        own = master.shape[1:]
        g = grads.reshape(nz, 8, width)
        hz = nz // 2
        f32, bf16 = jnp.float32, jnp.bfloat16
        dma = pltpu.SemaphoreType.DMA
        vmem = pl.BlockSpec(memory_space=pltpu.VMEM)
        out = pl.pallas_call(
            functools.partial(kernel, n_e, nz, quarter),
            out_shape=[jax.ShapeDtypeStruct(own, f32)] * 4 + [jax.ShapeDtypeStruct((nz, 8, width), bf16)],
            in_specs=[pl.BlockSpec(memory_space=pl.ANY), vmem, vmem, vmem],
            out_specs=[vmem] * 5,
            scratch_shapes=[
                pltpu.VMEM((nz, 8, 3 * quarter), bf16),
                pltpu.VMEM((nz, 8, quarter), bf16),
                pltpu.VMEM((2, nz, 8, 3 * half), bf16),
                pltpu.VMEM((2, nz, 8, half), bf16),
                pltpu.VMEM((2, hz + 1, 2, 8, half), f32),
                pltpu.VMEM((2, hz, 2, 8, half), f32),
                pltpu.VMEM((8, quarter), f32),
                pltpu.VMEM((NY, 2, quarter), f32),
                pltpu.VMEM((NY, 2, quarter), f32),
                pltpu.VMEM((3, NY, 2, quarter), f32),
                pltpu.VMEM((1, 128), f32),
                pltpu.VMEM((n_e * NY, 1, 128), f32),
                pltpu.VMEM((1, 128), f32),
                pltpu.VMEM((nz, 1, 128), f32),
                dma((NY,)), dma((1,)),
                dma((2, nz)), dma((2, nz)), dma((2, nz)), dma((2, nz)),
                dma((2, hz, 2)), dma((2, hz + 1, 2)),
                dma((4, NY)), dma((4, NY)),
                dma((n_e * NY,)), dma((n_e * NY,)), dma((nz,)), dma((nz,)),
                dma((2, hz + 1)), dma((2, hz + 1)),
                dma((2, nz)), dma((2, nz)), dma((2, nz)), dma((2, nz)),
            ],
            compiler_params=pltpu.CompilerParams(collective_id=0, has_side_effects=True),
        )(g, master.reshape(own), first.reshape(own), second.reshape(own))
        o_master, o_first, o_second, o_direction, w = out
        f = lambda a: a.reshape((1,) + own)
        return f(o_master), f(o_first), f(o_second), f(o_direction), w.reshape(1, rows, width)

    rows_spec = P("expert", "dp", None)
    return jax.shard_map(
        step,
        mesh=mesh,
        in_specs=(P("expert", "dp", None, None), rows_spec, rows_spec, rows_spec),
        out_specs=(rows_spec, rows_spec, rows_spec, rows_spec, P("expert", None, None)),
        check_vma=False,
    )
```

time: 363 us -> 99 us (0.27)
  the two profiles are of different devices: /device:TPU:4 before, /device:TPU:8 now
where the time goes in v1:
time: 99 us; the launch traced here: 98.6 us
  Pallas kernels  89.6 us (91%)
  local copies, waits for them, and re-layouts  8.37 us (8%)
    pallas_call x1, Pallas kernels, step(): pl.pallas_call(functools.partial(kernel, n_e, nz, quarter), out_shape=[ja...  89.6 us
    unnamed x5, local copies, waits for them, and re-layouts  8.37 us

profile of v1, /device:TPU:8, one launch (start us, length us, event | category | flops | bytes accessed | tf_op | source)
XLA Modules:
  0.0 98.6 jit_solution(4550557829812660786)
XLA Ops:
  0.6 89.6 %shard_map.83 = (f32[2,6144]{1,0:T(2,128)}, f32[2,6144]{1,0:T(2,128)}, f32[2,6144]{1,0:T(2,128)}, f32[2,6144]{1,0:T(2,128)}, bf16[16,8,6144]{2,1,0:T(8,128)(2,1)}) custom-call(bf16[16,8,6144]{2,1,0:T(8,128)(2,1)} %bitcast.10, f32[2,6144]{1,0:T(2,128)} %bitcast.15, f32[2,6144]{1,0:T(2,128)} %bitcast.16, f32[2,6144]{1,0:T(2,128)} %bitcast.17), custom_call_target="tpu_custom_call" | custom-call | tf_op jit(solution)/shard_map/pallas_call | solution.py:327
  90.2 1.4 %copy.14 = f32[1,2,6144]{2,1,0:T(2,128)} copy(f32[1,2,6144]{2,1,0:T(2,128)} %bitcast.14) | data formatting | bytes 98304
  91.7 1.4 %copy.15 = f32[1,2,6144]{2,1,0:T(2,128)} copy(f32[1,2,6144]{2,1,0:T(2,128)} %bitcast.13) | data formatting | bytes 98304
  93.1 1.4 %copy.16 = f32[1,2,6144]{2,1,0:T(2,128)} copy(f32[1,2,6144]{2,1,0:T(2,128)} %bitcast.12) | data formatting | bytes 98304
  94.5 1.4 %copy.17 = f32[1,2,6144]{2,1,0:T(2,128)} copy(f32[1,2,6144]{2,1,0:T(2,128)} %bitcast.11) | data formatting | bytes 98304
  95.9 2.7 %copy.18 = bf16[1,128,6144]{2,1,0:T(8,128)(2,1)} copy(bf16[1,128,6144]{2,1,0:T(8,128)(2,1)} %bitcast.9) | data formatting | bytes 3145728

commit v2 on v1

v2 whole, which is shorter than its diff:
```python
import functools

import jax
import jax.numpy as jnp
from jax import lax
from jax.experimental import pallas as pl
from jax.experimental.pallas import tpu as pltpu
from jax.sharding import PartitionSpec as P

STEP = 10
NY = 4
RS_STRIDE = 2
PARENT = {1: 0, 2: 0, 3: 1, 4: 2, 5: 3, 6: 4, 7: 5, 8: 6}
VMEM_LIMIT = 52 * 1024 * 1024
MESH = pl.DeviceIdType.MESH


def adam(clip, summed, master, first, second):
    clipped = clip * summed
    new_first = 0.9 * first + 0.1 * clipped
    new_second = 0.95 * second + 0.05 * (clipped * clipped)
    first_fix = 1.0 - 0.9**STEP
    second_fix = 1.0 - 0.95**STEP
    direction = new_first / first_fix / (jnp.sqrt(new_second / second_fix) + 1e-08)
    new_master = master - 0.001 * (direction + 0.1 * master)
    return new_master, new_first, new_second, direction


def kernel(
    n_e, nz, quarter,
    g_hbm, states_ref,
    outs, w_ref,
    g, yin, rin, zin, zout, total_q, s_out, s_in, t_in, norm_out, n1, norm2_out, n2,
    load_sem, send_sem, y_rsem, r_rsem, z_rsem, w_rsem, x_rsem, n1_rsem, n2_rsem,
):
    half = quarter // 2
    hz = nz // 2
    e = lax.axis_index("expert")
    d = lax.axis_index("dp")
    z = d // NY
    y = d % NY

    def at(zz, yy):
        return (e, ((zz + nz) % nz) * NY + (yy + NY) % NY)

    def columns(q):
        return pl.ds(pl.multiple_of(q * quarter, 128), quarter)

    for i in range(NY):
        pltpu.make_async_copy(
            g_hbm.at[:, :, columns((y + 1 + i) % NY)], g.at[:, :, pl.ds(i * quarter, quarter)], load_sem.at[0]).start()
    master_ref, first_ref, second_ref = (states_ref.at[a] for a in range(3))

    barrier = pltpu.get_barrier_semaphore()
    for dz in [sign * hop for hop in range(1, RS_STRIDE + 1) for sign in (1, -1)]:
        pl.semaphore_signal(barrier, inc=1, device_id=at(z + dz, y), device_id_type=MESH)

    peers = [((e + k) % n_e, (y + i) % NY) for k in range(n_e) for i in range(NY)][1:]
    for ee, yy in peers:
        pl.semaphore_signal(barrier, inc=1, device_id=(ee, z * NY + yy), device_id_type=MESH)
    pl.semaphore_wait(barrier, n_e * NY - 1 + 2 * RS_STRIDE)

    pltpu.make_async_copy(g, g, load_sem.at[0]).wait()

    def tile(j):
        i = (j + 1) // 2
        sign = 2 * (j % 2) - 1
        return (z + 2 * nz + sign * (hz - i)) % nz

    def y_copy(way, j):
        src = g.at[tile(j), :, pl.ds(way * 3 * half, 3 * half)]
        return pltpu.make_async_remote_copy(
            src_ref=src, dst_ref=yin.at[way, j], send_sem=send_sem.at[0], recv_sem=y_rsem.at[j],
            device_id=at(z, y + 1 - 2 * way), device_id_type=MESH)

    def relay(way, j):
        src = yin.at[way, j, :, pl.ds(2 * half if way == 0 else 0, half)]
        return pltpu.make_async_remote_copy(
            src_ref=src, dst_ref=rin.at[way, j], send_sem=send_sem.at[1], recv_sem=r_rsem.at[way, j],
            device_id=at(z, y + 1 - 2 * way), device_id_type=MESH)

    def z_copy(way, i, h, hop=RS_STRIDE):
        return pltpu.make_async_remote_copy(
            src_ref=zout.at[way, i, h], dst_ref=zin.at[way, i, h],
            send_sem=send_sem.at[2 + 7 * way], recv_sem=z_rsem.at[way, i, h],
            device_id=at(z + (1 - 2 * way) * hop, y), device_id_type=MESH)

    def arrive(j):
        pltpu.make_async_copy(yin.at[:, j], yin.at[:, j], y_rsem.at[j]).wait()
        for way in (0, 1):
            relay(way, j).start()

    def y_start(j):
        for way in (0, 1):
            y_copy(way, j).start()

    def y_sum(j, h):
        cols = pl.ds(h * half, half)
        own = g[tile(j), :, pl.ds(3 * quarter + h * half, half)].astype(jnp.float32)
        left = yin[0, j, :, cols].astype(jnp.float32)
        right = yin[1, j, :, pl.ds(half + h * half, half)].astype(jnp.float32)
        far = rin[h, j].astype(jnp.float32)
        return (own + left) + (right + far)

    def z_step(i, ways, begins, hop=RS_STRIDE):
        for h in (0, 1):
            for way in ways:
                j = 0 if isinstance(i, int) and i == 0 else 2 * i - 1 + way
                relay(h, j).wait_recv()
                value = y_sum(j, h)
                if not begins[way]:
                    z_copy(way, i - RS_STRIDE, h).wait_recv()
                    value = value + zin[way, i - RS_STRIDE, h]
                zout[way, i, h] = value
                z_copy(way, i, h, hop).start()

    def step(i):
        for j in (2 * i + 1, 2 * i + 2):
            if j < nz:
                arrive(j)
        for j in (2 * i + 5, 2 * i + 6):
            if j < nz:
                y_start(j)
        z_step(i, (0, 1) if i else (0,), tuple(i - RS_STRIDE < way for way in (0, 1)), min(RS_STRIDE, hz - i))

    for j in (0, 1, 2):
        y_start(j)

    arrive(0)
    for j in (3, 4):
        if j < nz:
            y_start(j)

    for i in range(min(3, hz - 1)):
        step(i)

    def middle(i, carry):
        arrive(2 * i + 1)
        arrive(2 * i + 2)
        pl.when(2 * i + 5 < nz)(lambda: y_start(2 * i + 5))
        pl.when(2 * i + 6 < nz)(lambda: y_start(2 * i + 6))
        z_step(i, (0, 1), (False, False))
        return carry

    lax.fori_loop(3, hz - 1, middle, 0)
    step(hz - 1)

    squares = jnp.zeros((8, half), jnp.float32)
    for h in (0, 1):
        relay(h, nz - 1).wait_recv()
        value = y_sum(nz - 1, h)
        for way in (0, 1):
            for i in range(max(hz - RS_STRIDE, way), hz):
                z_copy(way, i, h).wait_recv()
                value = value + zin[way, i, h]
        total_q[:, pl.ds(h * half, half)] = value
        squares = squares + value * value

    norm_out[...] = jnp.sum(jnp.sum(squares.reshape(8, half // 128, 128), axis=1), axis=0, keepdims=True)
    mine = e * NY + y
    n1[mine] = norm_out[...]

    def rows_of(ref, n):
        return ref.at[pl.ds(0, n)]

    for ee, yy in peers:
        pltpu.make_async_remote_copy(
            src_ref=norm_out, dst_ref=n1.at[mine], send_sem=send_sem.at[3], recv_sem=n1_rsem.at[0],
            device_id=(ee, z * NY + yy), device_id_type=MESH).start()

    for k in range(NY):
        s_out[k] = total_q[pl.ds(2 * k, 2), :]

    def x_copies(i):
        yy = (y + i) % NY
        copies = [pltpu.make_async_remote_copy(
            src_ref=s_out.at[yy], dst_ref=s_in.at[y], send_sem=send_sem.at[5], recv_sem=x_rsem.at[0],
            device_id=at(z, yy), device_id_type=MESH)]
        for a, ref in enumerate((master_ref, first_ref, second_ref)):
            copies.append(pltpu.make_async_remote_copy(
                src_ref=ref.at[:, columns(yy)], dst_ref=t_in.at[a, y],
                send_sem=send_sem.at[5], recv_sem=x_rsem.at[0],
                device_id=at(z, yy), device_id_type=MESH))
        return copies

    for i in range(1, NY):
        for copy in x_copies(i):
            copy.start()
    s_in[y] = s_out[y]
    for a, ref in enumerate((master_ref, first_ref, second_ref)):
        t_in[a, y] = ref[:, columns(y)]

    n1_rest = rows_of(n1, n_e * NY - 1)
    pltpu.make_async_copy(n1_rest, n1_rest, n1_rsem.at[0]).wait()

    norm2_out[...] = jnp.sum(n1[...], axis=0)
    n2[z] = norm2_out[...]

    for i in range(1, nz):
        pltpu.make_async_remote_copy(
            src_ref=norm2_out, dst_ref=n2.at[z], send_sem=send_sem.at[4], recv_sem=n2_rsem.at[0],
            device_id=at(z + i, y), device_id_type=MESH).start()

    pltpu.make_async_copy(t_in, t_in, x_rsem.at[0]).wait()

    n2_rest = rows_of(n2, nz - 1)
    pltpu.make_async_copy(n2_rest, n2_rest, n2_rsem.at[0]).wait()
    norm = jnp.sqrt(jnp.sum(jnp.sum(n2[...], axis=0), axis=1, keepdims=True))
    clip = 1.0 / jnp.maximum(norm, 1.0)

    states = [jnp.concatenate([t_in[a, k] for k in range(NY)], axis=0) for a in range(3)]
    w_ref[z, :, columns(y)] = adam(clip, total_q[...], *states)[0].astype(jnp.bfloat16)

    reach = (hz, hz - 1)

    def parent(way, t):
        return PARENT[t] if PARENT[t] <= reach[way] else 0

    def az_copy(way, t, hop):
        sign = 1 - 2 * way
        piece = w_ref.at[(z - sign * (t - hop) + nz) % nz, :, columns(y)]
        return pltpu.make_async_remote_copy(
            src_ref=piece, dst_ref=piece, send_sem=send_sem.at[6], recv_sem=z_rsem.at[way, t - 1, 0],
            device_id=at(z + sign * hop, y), device_id_type=MESH)

    def az_pass(way, t):
        for child in PARENT:
            if child <= reach[way] and parent(way, child) == t:
                az_copy(way, child, child - t).start()

    def ag_tile(j):
        t = (j + 1) // 2
        sign = 1 - 2 * (j % 2)
        return (z + nz + sign * t) % nz

    def ay_copy(way, j, forward):
        yy = y if forward else (y - 1 + 2 * way + NY) % NY
        piece = w_ref.at[ag_tile(j), :, columns(yy)]
        return pltpu.make_async_remote_copy(
            src_ref=piece, dst_ref=piece, send_sem=send_sem.at[7], recv_sem=y_rsem.at[j],
            device_id=at(z, y + 1 - 2 * way), device_id_type=MESH)

    def ar_copy(way, j, forward):
        q = ((y - 1 + 2 * way + NY) if forward else (y + 2)) % NY
        piece = w_ref.at[ag_tile(j), :, pl.ds(pl.multiple_of(q * quarter + way * half, 128), half)]
        return pltpu.make_async_remote_copy(
            src_ref=piece, dst_ref=piece, send_sem=send_sem.at[8], recv_sem=w_rsem.at[0],
            device_id=at(z, y + 1 - 2 * way), device_id_type=MESH)

    def y_out(j):
        for way in (0, 1):
            ay_copy(way, j, True).start()

    two = w_ref.at[pl.ds(0, 2), :, pl.ds(0, quarter)]

    def y_relay(j):
        pltpu.make_async_copy(two, two, y_rsem.at[j]).wait()
        for way in (0, 1):
            ar_copy(way, j, True).start()

    for way in (0, 1):
        az_pass(way, 0)
    y_out(0)

    for k in range(NY):
        cols = pl.ds(k * quarter, quarter)
        got = adam(clip, s_in[k], master_ref[:, cols], first_ref[:, cols], second_ref[:, cols])
        for a, value in enumerate(got):
            outs[a, :, cols] = value

    before = [0]
    for t in [t for t in PARENT if t <= hz]:
        here = []
        for way in (0, 1):
            if t <= reach[way]:
                az_copy(way, t, t - parent(way, t)).wait_recv()
                az_pass(way, t)
                here.append(2 * t - 1 + way)
                y_out(here[-1])
        for j in before:
            y_relay(j)
        before = here
    for j in before:
        y_relay(j)

    relayed = w_ref.at[:, :, pl.ds(0, quarter)]
    pltpu.make_async_copy(relayed, relayed, w_rsem.at[0]).wait()
    sent = (
        (0, yin), (1, rin), (2, zout.at[0]), (9, zout.at[1, pl.ds(1, hz - 1)]), (3, n1_rest), (4, n2_rest), (5, t_in),
        (6, w_ref.at[pl.ds(0, nz - 1), :, pl.ds(0, quarter)]), (7, w_ref.at[:, :, pl.ds(0, 2 * quarter)]), (8, relayed),
    )
    for i, ref in sent:
        pltpu.make_async_copy(ref, ref, send_sem.at[i]).wait()


def emit(outs, w, *refs):
    sem = refs[5]
    copies = [pltpu.make_async_copy(w, refs[4], sem.at[4])]
    copies += [pltpu.make_async_copy(outs.at[a], refs[a], sem.at[a]) for a in range(4)]
    for copy in copies:
        copy.start()
    for copy in copies:
        copy.wait()


def solution(mesh):
    n_e = mesh.shape["expert"]
    nz = mesh.shape["dp"] // NY

    def step(grads, master, first, second):
        rows, width = grads.shape[2:]
        quarter = width // NY
        half = quarter // 2
        own = master.shape[1:]
        g = grads.reshape(nz, 8, width)
        hz = nz // 2
        f32, bf16 = jnp.float32, jnp.bfloat16
        dma = pltpu.SemaphoreType.DMA
        hbm = pl.BlockSpec(memory_space=pltpu.HBM)
        vmem = pl.BlockSpec(memory_space=pltpu.VMEM)
        out = pl.pallas_call(
            functools.partial(kernel, n_e, nz, quarter),
            out_shape=[jax.ShapeDtypeStruct((4,) + own, f32), jax.ShapeDtypeStruct((nz, 8, width), bf16)],
            in_specs=[hbm, vmem],
            out_specs=[vmem] * 2,
            scratch_shapes=[
                pltpu.VMEM((nz, 8, width), bf16),
                pltpu.VMEM((2, nz, 8, 3 * half), bf16),
                pltpu.VMEM((2, nz, 8, half), bf16),
                pltpu.VMEM((2, hz, 2, 8, half), f32),
                pltpu.VMEM((2, hz, 2, 8, half), f32),
                pltpu.VMEM((8, quarter), f32),
                pltpu.VMEM((NY, 2, quarter), f32),
                pltpu.VMEM((NY, 2, quarter), f32),
                pltpu.VMEM((3, NY, 2, quarter), f32),
                pltpu.VMEM((1, 128), f32),
                pltpu.VMEM((n_e * NY, 1, 128), f32),
                pltpu.VMEM((1, 128), f32),
                pltpu.VMEM((nz, 1, 128), f32),
                dma((1,)), dma((10,)), dma((nz,)), dma((2, nz)), dma((2, hz, 2)), dma((1,)), dma((1,)), dma((1,)), dma((1,)),
            ],
            compiler_params=pltpu.CompilerParams(collective_id=0, has_side_effects=True, vmem_limit_bytes=VMEM_LIMIT),
        )(g, jnp.concatenate([master, first, second], axis=0))
        o_master, o_first, o_second, o_direction, w = pl.pallas_call(
            emit,
            out_shape=[jax.ShapeDtypeStruct(own, f32)] * 4 + [jax.ShapeDtypeStruct((nz, 8, width), bf16)],
            in_specs=[vmem] * 2,
            out_specs=[hbm] * 5,
            scratch_shapes=[dma((5,))],
            compiler_params=pltpu.CompilerParams(vmem_limit_bytes=VMEM_LIMIT),
        )(*out)
        f = lambda a: a.reshape((1,) + own)
        return f(o_master), f(o_first), f(o_second), f(o_direction), w.reshape(1, rows, width)

    rows_spec = P("expert", "dp", None)
    return jax.shard_map(
        step,
        mesh=mesh,
        in_specs=(P("expert", "dp", None, None), rows_spec, rows_spec, rows_spec),
        out_specs=(rows_spec, rows_spec, rows_spec, rows_spec, P("expert", None, None)),
        check_vma=False,
    )
```

time: 99 us -> 80.5 us (0.81)
  Pallas kernels: 89.6 us -> 78.8 us
  local copies, waits for them, and re-layouts: 8.37 us -> 0 us
    pallas_call x1, Pallas kernels: 89.6 us -> 77.6 us  [step(): pl.pallas_call(functools.partial(kernel, n_e, nz, quarter), out_shape=[ja...]
    unnamed x5 -> x0, local copies, waits for them, and re-layouts: 8.37 us -> none
    pallas_call x0 -> x1, Pallas kernels: none -> 1.23 us  [step(): pl.pallas_call(emit, out_shape=[jax.ShapeDtypeStruct(own, f32)] * 4 + [ja...]
where the time goes in v2:
time: 80.5 us; the launch traced here: 80.3 us
  Pallas kernels  78.8 us (98%)
  other arithmetic  0.92 us (1%)
    pallas_call x1, Pallas kernels, step(): pl.pallas_call(functools.partial(kernel, n_e, nz, quarter), out_shape=[ja...  77.6 us

profile of v2, /device:TPU:8, one launch (start us, length us, event | category | flops | bytes accessed | tf_op | source)
XLA Modules:
  0.0 80.3 jit_solution(15446161471635744143)
XLA Ops:
  0.6 0.9 %pad_maximum_fusion.states_ref = f32[3,2,6144]{2,1,0:T(2,128)S(1)} fusion(f32[1,2,6144]{2,1,0:T(2,128)} %param.7, f32[1,2,6144]{2,1,0:T(2,128)} %param.6, f32[1,2,6144]{2,1,0:T(2,128)} %param.5), kind=kLoop, calls=%fused_computation | loop fusion | flops 73728 | bytes 294912 | tf_op jit(solution)/shard_map/concatenate | solution.py:343
  1.6 77.6 %shard_map.83 = (f32[4,2,6144]{2,1,0:T(2,128)S(1)}, bf16[16,8,6144]{2,1,0:T(8,128)(2,1)S(1)}) custom-call(bf16[16,8,6144]{2,1,0:T(8,128)(2,1)} %bitcast.6, f32[3,2,6144]{2,1,0:T(2,128)S(1)} %pad_maximum_fusion.states_ref), custom_call_target="tpu_custom_call" | custom-call | tf_op jit(solution)/shard_map/pallas_call | solution.py:321
  79.1 1.2 %shard_map.84 = (f32[2,6144]{1,0:T(2,128)}, f32[2,6144]{1,0:T(2,128)}, f32[2,6144]{1,0:T(2,128)}, f32[2,6144]{1,0:T(2,128)}, bf16[16,8,6144]{2,1,0:T(8,128)(2,1)}) custom-call(f32[4,2,6144]{2,1,0:T(2,128)S(1)} %get-tuple-element.12.outs, bf16[16,8,6144]{2,1,0:T(8,128)(2,1)S(1)} %get-tuple-element.13.w), custom_call_target="tpu_custom_call" | custom-call | tf_op jit(solution)/shard_map/pallas_call | solution.py:344

commit v3 on v2

v3 whole, which is shorter than its diff:
```python
import functools

import jax
import jax.numpy as jnp
from jax import lax
from jax.experimental import pallas as pl
from jax.experimental.pallas import tpu as pltpu
from jax.sharding import PartitionSpec as P

STEP = 10
NY = 4
LEAD = 2
RS_ORDER = (8, 7, 5, 6, 4, 2, 3, 1)
RS_PARENT = {8: 6, 7: 6, 6: 3, 5: 3, 4: 3, 3: 0, 2: 0, 1: 0}
RS_REACH = max(t - p for t, p in RS_PARENT.items())
AG_LAG = 2
DIAGONAL = (7, 8)
PARENT = {2: 1, 3: 1, 4: 1, 5: 4, 6: 4, 7: 6, 8: 6}
VMEM_LIMIT = 52 * 1024 * 1024
MESH = pl.DeviceIdType.MESH


def adam(clip, summed, master, first, second):
    clipped = clip * summed
    new_first = 0.9 * first + 0.1 * clipped
    new_second = 0.95 * second + 0.05 * (clipped * clipped)
    first_fix = 1.0 - 0.9**STEP
    second_fix = 1.0 - 0.95**STEP
    direction = new_first / first_fix / (jnp.sqrt(new_second / second_fix) + 1e-08)
    new_master = master - 0.001 * (direction + 0.1 * master)
    return new_master, new_first, new_second, direction


def kernel(
    n_e, nz, quarter,
    g_hbm, states_ref,
    outs, w_ref,
    g, ain, bin_, rin, zin, zout, total_q, near, s_out, s_in, t_in, norm_out, n1, norm2_out, n2,
    load_sem, send_sem, a_rsem, b_rsem, r_rsem, y_rsem, z_rsem, w_rsem, x_rsem, t_rsem, near_rsem, q_rsem, n1_rsem, n2_rsem,
):
    half = quarter // 2
    hz = nz // 2
    e = lax.axis_index("expert")
    d = lax.axis_index("dp")
    z = d // NY
    y = d % NY

    def at(zz, yy):
        return (e, ((zz + nz) % nz) * NY + (yy + NY) % NY)

    def columns(q):
        return pl.ds(pl.multiple_of(q * quarter, 128), quarter)

    for i in range(NY):
        pltpu.make_async_copy(
            g_hbm.at[:, :, columns((y + 1 + i) % NY)], g.at[:, :, pl.ds(i * quarter, quarter)], load_sem.at[0]).start()

    barrier = pltpu.get_barrier_semaphore()
    for dz in [sign * hop for hop in range(1, RS_REACH + 1) for sign in (1, -1)]:
        pl.semaphore_signal(barrier, inc=1, device_id=at(z + dz, y), device_id_type=MESH)

    peers = [((e + k) % n_e, (y + i) % NY) for k in range(n_e) for i in range(NY)][1:]
    for ee, yy in peers:
        pl.semaphore_signal(barrier, inc=1, device_id=(ee, z * NY + yy), device_id_type=MESH)
    pl.semaphore_wait(barrier, n_e * NY - 1 + 2 * RS_REACH)

    pltpu.make_async_copy(g, g, load_sem.at[0]).wait()

    order = [t for t in RS_ORDER if t <= hz]
    reach = (hz, hz - 1)

    def children(way, t):
        return [order.index(c) for c in order if RS_PARENT[c] == t and c <= reach[way]]

    def tile(j):
        t = (order + [0])[(j + 1) // 2]
        return (z + nz + t * (2 * (j % 2) - 1 if j else 1)) % nz

    def tiles(i):
        return (0, 1) if i == 0 else (2 * i - 1, 1 if i == hz else 2)

    def y_send(way, j, i, src, dst, send, recv):
        pltpu.make_async_remote_copy(
            src_ref=src, dst_ref=dst, send_sem=send_sem.at[send], recv_sem=recv.at[i],
            device_id=at(z, y + 1 - 2 * way), device_id_type=MESH).start()

    def ahead(i):
        first, n = tiles(i)
        for k in range(n):
            for way in (0, 1):
                src = g.at[tile(first + k), :, pl.ds(quarter + way * half, half)]
                y_send(way, first + k, i, src, ain.at[way, first + k], 0, a_rsem)

    def direct(i):
        first, n = tiles(i)
        for k in range(n):
            for way in (0, 1):
                src = g.at[tile(first + k), :, pl.ds(2 * way * quarter, quarter)]
                y_send(way, first + k, i, src, bin_.at[way, first + k], 1, b_rsem)

    def arrived(i, ref, sem):
        first, n = tiles(i)
        piece = ref.at[:, pl.ds(first, n)]
        pltpu.make_async_copy(piece, piece, sem.at[i]).wait()

    def relay(i):
        arrived(i, ain, a_rsem)
        first, n = tiles(i)
        for k in range(n):
            for way in (0, 1):
                y_send(way, first + k, i, ain.at[way, first + k], rin.at[way, first + k], 8, r_rsem)

    def z_copy(way, i, h):
        hop = order[i] - RS_PARENT[order[i]]
        return pltpu.make_async_remote_copy(
            src_ref=zout.at[way, i, h], dst_ref=zin.at[way, i, h],
            send_sem=send_sem.at[2 + 7 * way], recv_sem=z_rsem.at[way, i, h],
            device_id=at(z + (1 - 2 * way) * hop, y), device_id_type=MESH)

    def add_arrived(value, way, t, h):
        for i in children(way, t):
            z_copy(way, i, h).wait_recv()
            value = value + zin[way, i, h]
        return value

    def y_sum(j, h):
        cols = pl.ds(h * half, half)
        own = g[tile(j), :, pl.ds(3 * quarter + h * half, half)].astype(jnp.float32)
        left = bin_[0, j, :, cols].astype(jnp.float32)
        right = bin_[1, j, :, cols].astype(jnp.float32)
        far = rin[h, j].astype(jnp.float32)
        return (own + left) + (right + far)

    def step(i):
        if i + LEAD <= hz:
            relay(i + LEAD)
        if i + 2 + LEAD <= hz:
            ahead(i + 2 + LEAD)
        if i + 2 <= hz:
            direct(i + 2)
        arrived(i, bin_, b_rsem)
        arrived(i, rin, r_rsem)
        for h in (0, 1):
            for way in (0, 1) if i else (0,):
                zout[way, i, h] = add_arrived(y_sum(tiles(i)[0] + way, h), way, order[i], h)
                z_copy(way, i, h).start()

    for way in (0, 1):
        pltpu.make_async_remote_copy(
            src_ref=states_ref, dst_ref=near.at[way], send_sem=send_sem.at[11], recv_sem=near_rsem.at[0],
            device_id=at(z + 1 - 2 * way, y), device_id_type=MESH).start()

    def give_states():
        pltpu.make_async_copy(near, near, near_rsem.at[0]).wait()
        for i in range(1, NY):
            yy = (y + i) % NY
            for src, dst, send in (
                (states_ref.at[:, :, columns(yy)], t_in.at[0, :, y], 12),
                (near.at[:, :, :, columns(yy)], t_in.at[pl.ds(1, 2), :, y], 13),
            ):
                pltpu.make_async_remote_copy(
                    src_ref=src, dst_ref=dst, send_sem=send_sem.at[send], recv_sem=t_rsem.at[0],
                    device_id=at(z, yy), device_id_type=MESH).start()
        for a in range(3):
            t_in[0, a, y] = states_ref[a, :, columns(y)]
            for way in (0, 1):
                t_in[1 + way, a, y] = near[way, a, :, columns(y)]

    for i in range(LEAD + 1):
        if i <= hz:
            ahead(i)
    direct(0)
    if LEAD + 1 <= hz:
        ahead(LEAD + 1)
    direct(1)

    for i in range(LEAD):
        if i <= hz:
            relay(i)

    for i in range(hz):
        step(i)
    give_states()

    squares = jnp.zeros((8, half), jnp.float32)
    arrived(hz, bin_, b_rsem)
    arrived(hz, rin, r_rsem)
    for h in (0, 1):
        value = y_sum(nz - 1, h)
        for way in (0, 1):
            value = add_arrived(value, way, 0, h)
        total_q[0, :, pl.ds(h * half, half)] = value
        squares = squares + value * value

    norm_out[...] = jnp.sum(jnp.sum(squares.reshape(8, half // 128, 128), axis=1), axis=0, keepdims=True)
    mine = e * NY + y
    n1[mine] = norm_out[...]

    def rows_of(ref, n):
        return ref.at[pl.ds(0, n)]

    for ee, yy in peers:
        pltpu.make_async_remote_copy(
            src_ref=norm_out, dst_ref=n1.at[mine], send_sem=send_sem.at[3], recv_sem=n1_rsem.at[0],
            device_id=(ee, z * NY + yy), device_id_type=MESH).start()

    for way in (0, 1):
        pltpu.make_async_remote_copy(
            src_ref=total_q.at[0], dst_ref=total_q.at[1 + way], send_sem=send_sem.at[14], recv_sem=q_rsem.at[0],
            device_id=at(z + 1 - 2 * way, y), device_id_type=MESH).start()
    for k in range(NY):
        s_out[k] = total_q[0, pl.ds(2 * k, 2), :]
    for i in range(1, NY):
        yy = (y + i) % NY
        pltpu.make_async_remote_copy(
            src_ref=s_out.at[yy], dst_ref=s_in.at[y], send_sem=send_sem.at[5], recv_sem=x_rsem.at[0],
            device_id=at(z, yy), device_id_type=MESH).start()
    s_in[y] = s_out[y]

    n1_rest = rows_of(n1, n_e * NY - 1)
    pltpu.make_async_copy(n1_rest, n1_rest, n1_rsem.at[0]).wait()

    norm2_out[...] = jnp.sum(n1[...], axis=0)
    n2[z] = norm2_out[...]

    for i in range(1, nz):
        pltpu.make_async_remote_copy(
            src_ref=norm2_out, dst_ref=n2.at[z], send_sem=send_sem.at[4], recv_sem=n2_rsem.at[0],
            device_id=at(z + i, y), device_id_type=MESH).start()

    s_rest, t_rest, q_rest = s_in.at[pl.ds(0, NY - 1)], t_in.at[:, :, pl.ds(0, NY - 1)], total_q.at[pl.ds(1, 2)]
    for ref, sem in ((s_rest, x_rsem), (t_rest, t_rsem), (q_rest, q_rsem)):
        pltpu.make_async_copy(ref, ref, sem.at[0]).wait()

    n2_rest = rows_of(n2, nz - 1)
    pltpu.make_async_copy(n2_rest, n2_rest, n2_rsem.at[0]).wait()
    norm = jnp.sqrt(jnp.sum(jnp.sum(n2[...], axis=0), axis=1, keepdims=True))
    clip = 1.0 / jnp.maximum(norm, 1.0)

    def update(c, carry):
        states = [jnp.concatenate([t_in[c, a, k] for k in range(NY)], axis=0) for a in range(3)]
        new = adam(clip, total_q[c], *states)[0]
        w_ref[(z + nz + c // 2 - c % 2) % nz, :, columns(y)] = new.astype(jnp.bfloat16)
        return carry

    lax.fori_loop(0, 3, update, 0)

    def az_copy(way, t, hop):
        sign = 1 - 2 * way
        piece = w_ref.at[(z - sign * (t - hop) + nz) % nz, :, columns(y)]
        return pltpu.make_async_remote_copy(
            src_ref=piece, dst_ref=piece, send_sem=send_sem.at[6], recv_sem=z_rsem.at[way, t - 1, 0],
            device_id=at(z + sign * hop, y), device_id_type=MESH)

    def diagonal(way, t, hop):
        sign = 1 - 2 * way
        piece = w_ref.at[(z - sign * (t - hop) + nz) % nz, :, columns(y)]
        j = 2 * t - 1 + way
        for i in (1, 3, 2):
            pltpu.make_async_remote_copy(
                src_ref=piece, dst_ref=piece, send_sem=send_sem.at[7 if i != 2 else 10],
                recv_sem=y_rsem.at[j] if i != 2 else w_rsem.at[0],
                device_id=at(z + sign * hop, y + i), device_id_type=MESH).start()

    def az_pass(way, t):
        for child in PARENT:
            if child <= reach[way] and PARENT[child] == t:
                az_copy(way, child, child - t).start()
                if child in DIAGONAL:
                    diagonal(way, child, child - t)

    def ag_tile(j):
        t = (j + 1) // 2
        sign = 1 - 2 * (j % 2)
        return (z + nz + sign * t) % nz

    def ay_copy(way, j, forward):
        yy = y if forward else (y - 1 + 2 * way + NY) % NY
        piece = w_ref.at[ag_tile(j), :, columns(yy)]
        return pltpu.make_async_remote_copy(
            src_ref=piece, dst_ref=piece, send_sem=send_sem.at[7], recv_sem=y_rsem.at[j],
            device_id=at(z, y + 1 - 2 * way), device_id_type=MESH)

    def ar_copy(way, j, forward):
        q = ((y - 1 + 2 * way + NY) if forward else (y + 2)) % NY
        piece = w_ref.at[ag_tile(j), :, pl.ds(pl.multiple_of(q * quarter + way * half, 128), half)]
        return pltpu.make_async_remote_copy(
            src_ref=piece, dst_ref=piece, send_sem=send_sem.at[10], recv_sem=w_rsem.at[0],
            device_id=at(z, y + 1 - 2 * way), device_id_type=MESH)

    def y_out(j):
        for way in (0, 1):
            ay_copy(way, j, True).start()

    two = w_ref.at[pl.ds(0, 2), :, pl.ds(0, quarter)]

    def y_relay(j):
        pltpu.make_async_copy(two, two, y_rsem.at[j]).wait()
        for way in (0, 1):
            ar_copy(way, j, True).start()

    for way in (0, 1):
        az_pass(way, 1)
    for j in range(3):
        y_out(j)

    for k in range(NY):
        cols = pl.ds(k * quarter, quarter)
        got = adam(clip, s_in[k], *[states_ref[a, :, cols] for a in range(3)])
        for a, value in enumerate(got):
            outs[a, :, cols] = value

    waiting, last = [[0, 1, 2]], []
    for t in [t for t in PARENT if t <= hz]:
        here = []
        for way in (0, 1):
            if t <= reach[way]:
                az_copy(way, t, t - PARENT[t]).wait_recv()
                az_pass(way, t)
                here.append(2 * t - 1 + way)
                if t in DIAGONAL:
                    last.append(here.pop())
                else:
                    y_out(here[-1])
        waiting.append(here)
        if len(waiting) > AG_LAG:
            for j in waiting.pop(0):
                y_relay(j)
    for j in sum(waiting, []):
        y_relay(j)
    for j in last:
        pltpu.make_async_copy(two, two, y_rsem.at[j]).wait()

    relayed = w_ref.at[:, :, pl.ds(0, quarter)]
    pltpu.make_async_copy(relayed, relayed, w_rsem.at[0]).wait()
    sent = (
        (0, ain), (1, bin_), (8, rin), (2, zout.at[0]), (9, zout.at[1, pl.ds(1, hz - 1)]), (3, n1_rest), (4, n2_rest), (5, s_rest), (11, near), (12, t_in.at[0, :, pl.ds(0, NY - 1)]),
        (13, t_in.at[pl.ds(1, 2), :, pl.ds(0, NY - 1)]), (14, q_rest),
        (6, w_ref.at[pl.ds(0, nz - 3), :, pl.ds(0, quarter)]), (7, w_ref.at[:, :, pl.ds(0, 2 * quarter)]), (10, relayed),
    )
    for i, ref in sent:
        pltpu.make_async_copy(ref, ref, send_sem.at[i]).wait()


def emit(outs, w, *refs):
    sem = refs[5]
    copies = [pltpu.make_async_copy(w, refs[4], sem.at[4])]
    copies += [pltpu.make_async_copy(outs.at[a], refs[a], sem.at[a]) for a in range(4)]
    for copy in copies:
        copy.start()
    for copy in copies:
        copy.wait()


def solution(mesh):
    n_e = mesh.shape["expert"]
    nz = mesh.shape["dp"] // NY

    def step(grads, master, first, second):
        rows, width = grads.shape[2:]
        quarter = width // NY
        half = quarter // 2
        own = master.shape[1:]
        g = grads.reshape(nz, 8, width)
        hz = nz // 2
        f32, bf16 = jnp.float32, jnp.bfloat16
        dma = pltpu.SemaphoreType.DMA
        hbm = pl.BlockSpec(memory_space=pltpu.HBM)
        vmem = pl.BlockSpec(memory_space=pltpu.VMEM)
        out = pl.pallas_call(
            functools.partial(kernel, n_e, nz, quarter),
            out_shape=[jax.ShapeDtypeStruct((4,) + own, f32), jax.ShapeDtypeStruct((nz, 8, width), bf16)],
            in_specs=[hbm, vmem],
            out_specs=[vmem] * 2,
            scratch_shapes=[
                pltpu.VMEM((nz, 8, width), bf16),
                pltpu.VMEM((2, nz, 8, half), bf16),
                pltpu.VMEM((2, nz, 8, quarter), bf16),
                pltpu.VMEM((2, nz, 8, half), bf16),
                pltpu.VMEM((2, hz, 2, 8, half), f32),
                pltpu.VMEM((2, hz, 2, 8, half), f32),
                pltpu.VMEM((3, 8, quarter), f32),
                pltpu.VMEM((2, 3) + own, f32),
                pltpu.VMEM((NY, 2, quarter), f32),
                pltpu.VMEM((NY, 2, quarter), f32),
                pltpu.VMEM((3, 3, NY, 2, quarter), f32),
                pltpu.VMEM((1, 128), f32),
                pltpu.VMEM((n_e * NY, 1, 128), f32),
                pltpu.VMEM((1, 128), f32),
                pltpu.VMEM((nz, 1, 128), f32),
                dma((1,)), dma((15,)), dma((hz + 1,)), dma((hz + 1,)), dma((hz + 1,)), dma((nz,)), dma((2, hz, 2)), *[dma((1,))] * 7,
            ],
            compiler_params=pltpu.CompilerParams(collective_id=0, has_side_effects=True, vmem_limit_bytes=VMEM_LIMIT),
        )(g, jnp.concatenate([master, first, second], axis=0))
        o_master, o_first, o_second, o_direction, w = pl.pallas_call(
            emit,
            out_shape=[jax.ShapeDtypeStruct(own, f32)] * 4 + [jax.ShapeDtypeStruct((nz, 8, width), bf16)],
            in_specs=[vmem] * 2,
            out_specs=[hbm] * 5,
            scratch_shapes=[dma((5,))],
            compiler_params=pltpu.CompilerParams(vmem_limit_bytes=VMEM_LIMIT),
        )(*out)
        f = lambda a: a.reshape((1,) + own)
        return f(o_master), f(o_first), f(o_second), f(o_direction), w.reshape(1, rows, width)

    rows_spec = P("expert", "dp", None)
    return jax.shard_map(
        step,
        mesh=mesh,
        in_specs=(P("expert", "dp", None, None), rows_spec, rows_spec, rows_spec),
        out_specs=(rows_spec, rows_spec, rows_spec, rows_spec, P("expert", None, None)),
        check_vma=False,
    )
```

time: 80.5 us -> 73.5 us (0.913)
  the two profiles are of different devices: /device:TPU:8 before, /device:TPU:2 now
where the time goes in v3:
time: 73.5 us; the launch traced here: 73.4 us
  Pallas kernels  71.8 us (98%)
  other arithmetic  0.92 us (1%)
    pallas_call x1, Pallas kernels, step(): pl.pallas_call(functools.partial(kernel, n_e, nz, quarter), out_shape=[ja...  70.6 us

profile of v3, /device:TPU:2, one launch (start us, length us, event | category | flops | bytes accessed | tf_op | source)
XLA Modules:
  0.0 73.4 jit_solution(1728105186874085931)
XLA Ops:
  0.6 0.9 %pad_maximum_fusion.states_ref = f32[3,2,6144]{2,1,0:T(2,128)S(1)} fusion(f32[1,2,6144]{2,1,0:T(2,128)} %param.7, f32[1,2,6144]{2,1,0:T(2,128)} %param.6, f32[1,2,6144]{2,1,0:T(2,128)} %param.5), kind=kLoop, calls=%fused_computation | loop fusion | flops 73728 | bytes 294912 | tf_op jit(solution)/shard_map/concatenate | solution.py:394
  1.6 70.6 %shard_map.83 = (f32[4,2,6144]{2,1,0:T(2,128)S(1)}, bf16[16,8,6144]{2,1,0:T(8,128)(2,1)S(1)}) custom-call(bf16[16,8,6144]{2,1,0:T(8,128)(2,1)} %bitcast.6, f32[3,2,6144]{2,1,0:T(2,128)S(1)} %pad_maximum_fusion.states_ref), custom_call_target="tpu_custom_call" | custom-call | tf_op jit(solution)/shard_map/pallas_call | solution.py:370
  72.1 1.2 %shard_map.84 = (f32[2,6144]{1,0:T(2,128)}, f32[2,6144]{1,0:T(2,128)}, f32[2,6144]{1,0:T(2,128)}, f32[2,6144]{1,0:T(2,128)}, bf16[16,8,6144]{2,1,0:T(8,128)(2,1)}) custom-call(f32[4,2,6144]{2,1,0:T(2,128)S(1)} %get-tuple-element.12.outs, bf16[16,8,6144]{2,1,0:T(8,128)(2,1)S(1)} %get-tuple-element.13.w), custom_call_target="tpu_custom_call" | custom-call | tf_op jit(solution)/shard_map/pallas_call | solution.py:395

commit v4 on v3

--- a/solution.py
+++ b/solution.py
@@ -12,7 +12,7 @@
 LEAD = 2
 RS_ORDER = (8, 7, 5, 6, 4, 2, 3, 1)
 RS_PARENT = {8: 6, 7: 6, 6: 3, 5: 3, 4: 3, 3: 0, 2: 0, 1: 0}
-RS_REACH = max(t - p for t, p in RS_PARENT.items())
+ROUNDS = 4
 AG_LAG = 2
 DIAGONAL = (7, 8)
 PARENT = {2: 1, 3: 1, 4: 1, 5: 4, 6: 4, 7: 6, 8: 6}
@@ -36,7 +36,7 @@
     g_hbm, states_ref,
     outs, w_ref,
     g, ain, bin_, rin, zin, zout, total_q, near, s_out, s_in, t_in, norm_out, n1, norm2_out, n2,
-    load_sem, send_sem, a_rsem, b_rsem, r_rsem, y_rsem, z_rsem, w_rsem, x_rsem, t_rsem, near_rsem, q_rsem, n1_rsem, n2_rsem,
+    load_sem, send_sem, a_rsem, b_rsem, r_rsem, y_rsem, z_rsem, w_rsem, x_rsem, t_rsem, near_rsem, q_rsem, n1_rsem, n2_rsem, met,
 ):
     half = quarter // 2
     hz = nz // 2
@@ -55,14 +55,27 @@
         pltpu.make_async_copy(
             g_hbm.at[:, :, columns((y + 1 + i) % NY)], g.at[:, :, pl.ds(i * quarter, quarter)], load_sem.at[0]).start()
 
+    def other(ee):
+        return ((ee + n_e) % n_e, d)
+
+    neighbours = [at(z + 1, y), at(z - 1, y), at(z, y + 1), at(z, y - 1), other(e + 1 - 2 * (e % 2))]
+    if n_e > 2:
+        neighbours += [other(e + 2), other(e - 2)]
+
+    def greet(sem):
+        for device in neighbours:
+            pl.semaphore_signal(sem, inc=1, device_id=device, device_id_type=MESH)
+
     barrier = pltpu.get_barrier_semaphore()
-    for dz in [sign * hop for hop in range(1, RS_REACH + 1) for sign in (1, -1)]:
-        pl.semaphore_signal(barrier, inc=1, device_id=at(z + dz, y), device_id_type=MESH)
-
-    peers = [((e + k) % n_e, (y + i) % NY) for k in range(n_e) for i in range(NY)][1:]
-    for ee, yy in peers:
-        pl.semaphore_signal(barrier, inc=1, device_id=(ee, z * NY + yy), device_id_type=MESH)
-    pl.semaphore_wait(barrier, n_e * NY - 1 + 2 * RS_REACH)
+    greet(barrier)
+    pl.semaphore_wait(barrier, len(neighbours))
+
+    def round_(r):
+        pl.semaphore_wait(met.at[r], len(neighbours))
+        if r + 1 < ROUNDS:
+            greet(met.at[r + 1])
+
+    greet(met.at[0])
 
     pltpu.make_async_copy(g, g, load_sem.at[0]).wait()
 
@@ -132,6 +145,8 @@
         return (own + left) + (right + far)
 
     def step(i):
+        if i < ROUNDS:
+            round_(i)
         if i + LEAD <= hz:
             relay(i + LEAD)
         if i + 2 + LEAD <= hz:
@@ -196,13 +211,20 @@
     mine = e * NY + y
     n1[mine] = norm_out[...]
 
-    def rows_of(ref, n):
-        return ref.at[pl.ds(0, n)]
-
-    for ee, yy in peers:
+    def far_first(n):
+        return sorted(range(n), key=lambda i: -min(i, n - i))
+
+    def n1_send(k, i):
+        ee = ((e // 2 + k) % (n_e // 2)) * 2 + 1
         pltpu.make_async_remote_copy(
             src_ref=norm_out, dst_ref=n1.at[mine], send_sem=send_sem.at[3], recv_sem=n1_rsem.at[0],
-            device_id=(ee, z * NY + yy), device_id_type=MESH).start()
+            device_id=(ee, z * NY + (y + i) % NY), device_id_type=MESH).start()
+
+    for k in far_first(n_e // 2):
+        for i in far_first(NY):
+            if k or i:
+                n1_send(k, i)
+    pl.when(e % 2 == 0)(lambda: n1_send(0, 0))
 
     for way in (0, 1):
         pltpu.make_async_remote_copy(
@@ -217,23 +239,31 @@
             device_id=at(z, yy), device_id_type=MESH).start()
     s_in[y] = s_out[y]
 
-    n1_rest = rows_of(n1, n_e * NY - 1)
-    pltpu.make_async_copy(n1_rest, n1_rest, n1_rsem.at[0]).wait()
-
-    norm2_out[...] = jnp.sum(n1[...], axis=0)
-    n2[z] = norm2_out[...]
-
-    for i in range(1, nz):
+    def wait_rows(ref, n, sem):
+        piece = ref.at[pl.ds(0, n)]
+        pltpu.make_async_copy(piece, piece, sem).wait()
+
+    def n2_send(i, core):
         pltpu.make_async_remote_copy(
             src_ref=norm2_out, dst_ref=n2.at[z], send_sem=send_sem.at[4], recv_sem=n2_rsem.at[0],
-            device_id=at(z + i, y), device_id_type=MESH).start()
+            device_id=(e - 1 + core, ((z + i) % nz) * NY + y), device_id_type=MESH).start()
+
+    @pl.when(e % 2 == 1)
+    def _():
+        wait_rows(n1, n_e * NY - 1, n1_rsem.at[0])
+        norm2_out[...] = jnp.sum(n1[...], axis=0)
+        n2[z] = norm2_out[...]
+        for i in far_first(nz):
+            n2_send(i, 0)
+            if i:
+                n2_send(i, 1)
 
     s_rest, t_rest, q_rest = s_in.at[pl.ds(0, NY - 1)], t_in.at[:, :, pl.ds(0, NY - 1)], total_q.at[pl.ds(1, 2)]
     for ref, sem in ((s_rest, x_rsem), (t_rest, t_rsem), (q_rest, q_rsem)):
         pltpu.make_async_copy(ref, ref, sem.at[0]).wait()
 
-    n2_rest = rows_of(n2, nz - 1)
-    pltpu.make_async_copy(n2_rest, n2_rest, n2_rsem.at[0]).wait()
+    pl.when(e % 2 == 1)(lambda: wait_rows(n2, nz - 1, n2_rsem.at[0]))
+    pl.when(e % 2 == 0)(lambda: wait_rows(n2, nz, n2_rsem.at[0]))
     norm = jnp.sqrt(jnp.sum(jnp.sum(n2[...], axis=0), axis=1, keepdims=True))
     clip = 1.0 / jnp.maximum(norm, 1.0)
 
@@ -263,11 +293,13 @@
                 device_id=at(z + sign * hop, y + i), device_id_type=MESH).start()
 
     def az_pass(way, t):
-        for child in PARENT:
-            if child <= reach[way] and PARENT[child] == t:
-                az_copy(way, child, child - t).start()
-                if child in DIAGONAL:
-                    diagonal(way, child, child - t)
+        far = [c for c in PARENT if PARENT[c] == t and c <= reach[way]]
+        if t == 6:
+            far = far[::-1]
+        for child in far:
+            if child in DIAGONAL:
+                diagonal(way, child, child - t)
+            az_copy(way, child, child - t).start()
 
     def ag_tile(j):
         t = (j + 1) // 2
@@ -310,34 +342,40 @@
         for a, value in enumerate(got):
             outs[a, :, cols] = value
 
-    waiting, last = [[0, 1, 2]], []
+    waiting, leaves = [[0, 1, 2]], []
     for t in [t for t in PARENT if t <= hz]:
         here = []
         for way in (0, 1):
-            if t <= reach[way]:
-                az_copy(way, t, t - PARENT[t]).wait_recv()
-                az_pass(way, t)
-                here.append(2 * t - 1 + way)
-                if t in DIAGONAL:
-                    last.append(here.pop())
-                else:
-                    y_out(here[-1])
-        waiting.append(here)
-        if len(waiting) > AG_LAG:
-            for j in waiting.pop(0):
-                y_relay(j)
+            if t > reach[way]:
+                continue
+            if t in DIAGONAL:
+                leaves.append((way, t))
+                continue
+            az_copy(way, t, t - PARENT[t]).wait_recv()
+            az_pass(way, t)
+            here.append(2 * t - 1 + way)
+            y_out(here[-1])
+        if here:
+            waiting.append(here)
+            if len(waiting) > AG_LAG:
+                for j in waiting.pop(0):
+                    y_relay(j)
     for j in sum(waiting, []):
         y_relay(j)
-    for j in last:
-        pltpu.make_async_copy(two, two, y_rsem.at[j]).wait()
+    for way, t in leaves:
+        az_copy(way, t, t - PARENT[t]).wait_recv()
+        pltpu.make_async_copy(two, two, y_rsem.at[2 * t - 1 + way]).wait()
 
     relayed = w_ref.at[:, :, pl.ds(0, quarter)]
     pltpu.make_async_copy(relayed, relayed, w_rsem.at[0]).wait()
     sent = (
-        (0, ain), (1, bin_), (8, rin), (2, zout.at[0]), (9, zout.at[1, pl.ds(1, hz - 1)]), (3, n1_rest), (4, n2_rest), (5, s_rest), (11, near), (12, t_in.at[0, :, pl.ds(0, NY - 1)]),
+        (0, ain), (1, bin_), (8, rin), (2, zout.at[0]), (9, zout.at[1, pl.ds(1, hz - 1)]), (5, s_rest), (11, near), (12, t_in.at[0, :, pl.ds(0, NY - 1)]),
         (13, t_in.at[pl.ds(1, 2), :, pl.ds(0, NY - 1)]), (14, q_rest),
         (6, w_ref.at[pl.ds(0, nz - 3), :, pl.ds(0, quarter)]), (7, w_ref.at[:, :, pl.ds(0, 2 * quarter)]), (10, relayed),
     )
+    wait_rows(n1, n_e * NY // 2 - 1, send_sem.at[3])
+    pl.when(e % 2 == 0)(lambda: wait_rows(n1, 1, send_sem.at[3]))
+    pl.when(e % 2 == 1)(lambda: wait_rows(n1, 2 * nz - 1, send_sem.at[4]))
     for i, ref in sent:
         pltpu.make_async_copy(ref, ref, send_sem.at[i]).wait()
 
@@ -388,7 +426,7 @@
                 pltpu.VMEM((n_e * NY, 1, 128), f32),
                 pltpu.VMEM((1, 128), f32),
                 pltpu.VMEM((nz, 1, 128), f32),
-                dma((1,)), dma((15,)), dma((hz + 1,)), dma((hz + 1,)), dma((hz + 1,)), dma((nz,)), dma((2, hz, 2)), *[dma((1,))] * 7,
+                dma((1,)), dma((15,)), dma((hz + 1,)), dma((hz + 1,)), dma((hz + 1,)), dma((nz,)), dma((2, hz, 2)), *[dma((1,))] * 7, pltpu.SemaphoreType.REGULAR((ROUNDS,)),
             ],
             compiler_params=pltpu.CompilerParams(collective_id=0, has_side_effects=True, vmem_limit_bytes=VMEM_LIMIT),
         )(g, jnp.concatenate([master, first, second], axis=0))

time: 73.5 us -> 72.5 us (0.986)
  the two profiles are of different devices: /device:TPU:2 before, /device:TPU:32 now
where the time goes in v4:
time: 72.5 us; the launch traced here: 72.3 us
  Pallas kernels  70.8 us (98%)
  other arithmetic  0.92 us (1%)
    pallas_call x1, Pallas kernels, step(): pl.pallas_call(functools.partial(kernel, n_e, nz, quarter), out_shape=[ja...  69.5 us

profile of v4, /device:TPU:32, one launch (start us, length us, event | category | flops | bytes accessed | tf_op | source)
XLA Modules:
  0.0 72.3 jit_solution(7384296654326763513)
XLA Ops:
  0.6 0.9 %pad_maximum_fusion.states_ref = f32[3,2,6144]{2,1,0:T(2,128)S(1)} fusion(f32[1,2,6144]{2,1,0:T(2,128)} %param.7, f32[1,2,6144]{2,1,0:T(2,128)} %param.6, f32[1,2,6144]{2,1,0:T(2,128)} %param.5), kind=kLoop, calls=%fused_computation | loop fusion | flops 73728 | bytes 294912 | tf_op jit(solution)/shard_map/concatenate | solution.py:432
  1.6 69.5 %shard_map.83 = (f32[4,2,6144]{2,1,0:T(2,128)S(1)}, bf16[16,8,6144]{2,1,0:T(8,128)(2,1)S(1)}) custom-call(bf16[16,8,6144]{2,1,0:T(8,128)(2,1)} %bitcast.6, f32[3,2,6144]{2,1,0:T(2,128)S(1)} %pad_maximum_fusion.states_ref), custom_call_target="tpu_custom_call" | custom-call | tf_op jit(solution)/shard_map/pallas_call | solution.py:408
  71.1 1.2 %shard_map.84 = (f32[2,6144]{1,0:T(2,128)}, f32[2,6144]{1,0:T(2,128)}, f32[2,6144]{1,0:T(2,128)}, f32[2,6144]{1,0:T(2,128)}, bf16[16,8,6144]{2,1,0:T(8,128)(2,1)}) custom-call(f32[4,2,6144]{2,1,0:T(2,128)S(1)} %get-tuple-element.12.outs, bf16[16,8,6144]{2,1,0:T(8,128)(2,1)S(1)} %get-tuple-element.13.w), custom_call_target="tpu_custom_call" | custom-call | tf_op jit(solution)/shard_map/pallas_call | solution.py:433

commit v5 on v4

--- a/solution.py
+++ b/solution.py
@@ -9,7 +9,7 @@
 
 STEP = 10
 NY = 4
-LEAD = 2
+LEAD = 1
 RS_ORDER = (8, 7, 5, 6, 4, 2, 3, 1)
 RS_PARENT = {8: 6, 7: 6, 6: 3, 5: 3, 4: 3, 3: 0, 2: 0, 1: 0}
 ROUNDS = 4

time: 72.5 us -> 72.1 us (level)
  no operation moved by 1% of the time
where the time goes in v5:
time: 72.1 us; the launch traced here: 72 us
  Pallas kernels  70.4 us (98%)
  other arithmetic  0.92 us (1%)
    pallas_call x1, Pallas kernels, step(): pl.pallas_call(functools.partial(kernel, n_e, nz, quarter), out_shape=[ja...  69.2 us

profile of v5, /device:TPU:32, one launch (start us, length us, event | category | flops | bytes accessed | tf_op | source)
XLA Modules:
  0.0 72.0 jit_solution(1838554134604835284)
XLA Ops:
  0.6 0.9 %pad_maximum_fusion.states_ref = f32[3,2,6144]{2,1,0:T(2,128)S(1)} fusion(f32[1,2,6144]{2,1,0:T(2,128)} %param.7, f32[1,2,6144]{2,1,0:T(2,128)} %param.6, f32[1,2,6144]{2,1,0:T(2,128)} %param.5), kind=kLoop, calls=%fused_computation | loop fusion | flops 73728 | bytes 294912 | tf_op jit(solution)/shard_map/concatenate | solution.py:432
  1.6 69.2 %shard_map.83 = (f32[4,2,6144]{2,1,0:T(2,128)S(1)}, bf16[16,8,6144]{2,1,0:T(8,128)(2,1)S(1)}) custom-call(bf16[16,8,6144]{2,1,0:T(8,128)(2,1)} %bitcast.6, f32[3,2,6144]{2,1,0:T(2,128)S(1)} %pad_maximum_fusion.states_ref), custom_call_target="tpu_custom_call" | custom-call | tf_op jit(solution)/shard_map/pallas_call | solution.py:408
  70.7 1.2 %shard_map.84 = (f32[2,6144]{1,0:T(2,128)}, f32[2,6144]{1,0:T(2,128)}, f32[2,6144]{1,0:T(2,128)}, f32[2,6144]{1,0:T(2,128)}, bf16[16,8,6144]{2,1,0:T(8,128)(2,1)}) custom-call(f32[4,2,6144]{2,1,0:T(2,128)S(1)} %get-tuple-element.12.outs, bf16[16,8,6144]{2,1,0:T(8,128)(2,1)S(1)} %get-tuple-element.13.w), custom_call_target="tpu_custom_call" | custom-call | tf_op jit(solution)/shard_map/pallas_call | solution.py:433

commit v6 on v5

--- a/solution.py
+++ b/solution.py
@@ -36,10 +36,11 @@
     g_hbm, states_ref,
     outs, w_ref,
     g, ain, bin_, rin, zin, zout, total_q, near, s_out, s_in, t_in, norm_out, n1, norm2_out, n2,
-    load_sem, send_sem, a_rsem, b_rsem, r_rsem, y_rsem, z_rsem, w_rsem, x_rsem, t_rsem, near_rsem, q_rsem, n1_rsem, n2_rsem, met,
+    load_sem, send_sem, y_rsem, r_rsem, z_rsem, w_rsem, x_rsem, t_rsem, near_rsem, q_rsem, n1_rsem, n2_rsem, met,
 ):
     half = quarter // 2
     hz = nz // 2
+    a_rsem, b_rsem = y_rsem.at[pl.ds(0, hz + 1)], y_rsem.at[pl.ds(hz + 1, hz + 1)]
     e = lax.axis_index("expert")
     d = lax.axis_index("dp")
     z = d // NY
@@ -109,7 +110,7 @@
         for k in range(n):
             for way in (0, 1):
                 src = g.at[tile(first + k), :, pl.ds(2 * way * quarter, quarter)]
-                y_send(way, first + k, i, src, bin_.at[way, first + k], 1, b_rsem)
+                y_send(way, first + k, i, src, bin_.at[way, first + k], 0, b_rsem)
 
     def arrived(i, ref, sem):
         first, n = tiles(i)
@@ -121,7 +122,7 @@
         first, n = tiles(i)
         for k in range(n):
             for way in (0, 1):
-                y_send(way, first + k, i, ain.at[way, first + k], rin.at[way, first + k], 8, r_rsem)
+                y_send(way, first + k, i, ain.at[way, first + k], rin.at[way, first + k], 0, r_rsem)
 
     def z_copy(way, i, h):
         hop = order[i] - RS_PARENT[order[i]]
@@ -162,7 +163,7 @@
 
     for way in (0, 1):
         pltpu.make_async_remote_copy(
-            src_ref=states_ref, dst_ref=near.at[way], send_sem=send_sem.at[11], recv_sem=near_rsem.at[0],
+            src_ref=states_ref, dst_ref=near.at[way], send_sem=send_sem.at[8], recv_sem=near_rsem.at[0],
             device_id=at(z + 1 - 2 * way, y), device_id_type=MESH).start()
 
     def give_states():
@@ -170,8 +171,8 @@
         for i in range(1, NY):
             yy = (y + i) % NY
             for src, dst, send in (
-                (states_ref.at[:, :, columns(yy)], t_in.at[0, :, y], 12),
-                (near.at[:, :, :, columns(yy)], t_in.at[pl.ds(1, 2), :, y], 13),
+                (states_ref.at[:, :, columns(yy)], t_in.at[0, :, y], 1),
+                (near.at[:, :, :, columns(yy)], t_in.at[pl.ds(1, 2), :, y], 1),
             ):
                 pltpu.make_async_remote_copy(
                     src_ref=src, dst_ref=dst, send_sem=send_sem.at[send], recv_sem=t_rsem.at[0],
@@ -228,7 +229,7 @@
 
     for way in (0, 1):
         pltpu.make_async_remote_copy(
-            src_ref=total_q.at[0], dst_ref=total_q.at[1 + way], send_sem=send_sem.at[14], recv_sem=q_rsem.at[0],
+            src_ref=total_q.at[0], dst_ref=total_q.at[1 + way], send_sem=send_sem.at[10], recv_sem=q_rsem.at[0],
             device_id=at(z + 1 - 2 * way, y), device_id_type=MESH).start()
     for k in range(NY):
         s_out[k] = total_q[0, pl.ds(2 * k, 2), :]
@@ -288,7 +289,7 @@
         j = 2 * t - 1 + way
         for i in (1, 3, 2):
             pltpu.make_async_remote_copy(
-                src_ref=piece, dst_ref=piece, send_sem=send_sem.at[7 if i != 2 else 10],
+                src_ref=piece, dst_ref=piece, send_sem=send_sem.at[7],
                 recv_sem=y_rsem.at[j] if i != 2 else w_rsem.at[0],
                 device_id=at(z + sign * hop, y + i), device_id_type=MESH).start()
 
@@ -317,7 +318,7 @@
         q = ((y - 1 + 2 * way + NY) if forward else (y + 2)) % NY
         piece = w_ref.at[ag_tile(j), :, pl.ds(pl.multiple_of(q * quarter + way * half, 128), half)]
         return pltpu.make_async_remote_copy(
-            src_ref=piece, dst_ref=piece, send_sem=send_sem.at[10], recv_sem=w_rsem.at[0],
+            src_ref=piece, dst_ref=piece, send_sem=send_sem.at[7], recv_sem=w_rsem.at[0],
             device_id=at(z, y + 1 - 2 * way), device_id_type=MESH)
 
     def y_out(j):
@@ -369,9 +370,8 @@
     relayed = w_ref.at[:, :, pl.ds(0, quarter)]
     pltpu.make_async_copy(relayed, relayed, w_rsem.at[0]).wait()
     sent = (
-        (0, ain), (1, bin_), (8, rin), (2, zout.at[0]), (9, zout.at[1, pl.ds(1, hz - 1)]), (5, s_rest), (11, near), (12, t_in.at[0, :, pl.ds(0, NY - 1)]),
-        (13, t_in.at[pl.ds(1, 2), :, pl.ds(0, NY - 1)]), (14, q_rest),
-        (6, w_ref.at[pl.ds(0, nz - 3), :, pl.ds(0, quarter)]), (7, w_ref.at[:, :, pl.ds(0, 2 * quarter)]), (10, relayed),
+        (0, g), (1, t_rest), (2, zout.at[0]), (9, zout.at[1, pl.ds(1, hz - 1)]), (5, s_rest),
+        (6, w_ref.at[pl.ds(0, nz - 3), :, pl.ds(0, quarter)]), (7, w_ref.at[:, :, pl.ds(0, 3 * quarter)]), (8, near), (10, q_rest),
     )
     wait_rows(n1, n_e * NY // 2 - 1, send_sem.at[3])
     pl.when(e % 2 == 0)(lambda: wait_rows(n1, 1, send_sem.at[3]))
@@ -426,7 +426,7 @@
                 pltpu.VMEM((n_e * NY, 1, 128), f32),
                 pltpu.VMEM((1, 128), f32),
                 pltpu.VMEM((nz, 1, 128), f32),
-                dma((1,)), dma((15,)), dma((hz + 1,)), dma((hz + 1,)), dma((hz + 1,)), dma((nz,)), dma((2, hz, 2)), *[dma((1,))] * 7, pltpu.SemaphoreType.REGULAR((ROUNDS,)),
+                dma((1,)), dma((11,)), dma((2 * hz + 2,)), dma((hz + 1,)), dma((2, hz, 2)), *[dma((1,))] * 7, pltpu.SemaphoreType.REGULAR((ROUNDS,)),
             ],
             compiler_params=pltpu.CompilerParams(collective_id=0, has_side_effects=True, vmem_limit_bytes=VMEM_LIMIT),
         )(g, jnp.concatenate([master, first, second], axis=0))

time: 72.1 us -> 72 us (level)
  no operation moved by 1% of the time
where the time goes in v6:
time: 72 us; the launch traced here: 71.8 us
  Pallas kernels  70.2 us (98%)
  other arithmetic  0.92 us (1%)
    pallas_call x1, Pallas kernels, step(): pl.pallas_call(functools.partial(kernel, n_e, nz, quarter), out_shape=[ja...  69 us

profile of v6, /device:TPU:32, one launch (start us, length us, event | category | flops | bytes accessed | tf_op | source)
XLA Modules:
  0.0 71.8 jit_solution(7217832792256648557)
XLA Ops:
  0.6 0.9 %pad_maximum_fusion.states_ref = f32[3,2,6144]{2,1,0:T(2,128)S(1)} fusion(f32[1,2,6144]{2,1,0:T(2,128)} %param.7, f32[1,2,6144]{2,1,0:T(2,128)} %param.6, f32[1,2,6144]{2,1,0:T(2,128)} %param.5), kind=kLoop, calls=%fused_computation | loop fusion | flops 73728 | bytes 294912 | tf_op jit(solution)/shard_map/concatenate | solution.py:432
  1.6 69.0 %shard_map.83 = (f32[4,2,6144]{2,1,0:T(2,128)S(1)}, bf16[16,8,6144]{2,1,0:T(8,128)(2,1)S(1)}) custom-call(bf16[16,8,6144]{2,1,0:T(8,128)(2,1)} %bitcast.6, f32[3,2,6144]{2,1,0:T(2,128)S(1)} %pad_maximum_fusion.states_ref), custom_call_target="tpu_custom_call" | custom-call | tf_op jit(solution)/shard_map/pallas_call | solution.py:408
  70.5 1.2 %shard_map.84 = (f32[2,6144]{1,0:T(2,128)}, f32[2,6144]{1,0:T(2,128)}, f32[2,6144]{1,0:T(2,128)}, f32[2,6144]{1,0:T(2,128)}, bf16[16,8,6144]{2,1,0:T(8,128)(2,1)}) custom-call(f32[4,2,6144]{2,1,0:T(2,128)S(1)} %get-tuple-element.12.outs, bf16[16,8,6144]{2,1,0:T(8,128)(2,1)S(1)} %get-tuple-element.13.w), custom_call_target="tpu_custom_call" | custom-call | tf_op jit(solution)/shard_map/pallas_call | solution.py:433
